TPU v7x, 128 devices: a whole 4x4x4 slice. The times are simulated.
128 devices in a mesh: replica: 64 (over z, y, x), fsdp: 2 (over core).
Axes of the slice: x: 4, y: 4, z: 4, core: 2. Of those that a mesh axis runs over, the one named last changes fastest.
Arguments:
- block_in: bfloat16 [1, 131072, 896], P(None, ('replica', 'fsdp'))
- grad_out: bfloat16 [131072, 896], P(('replica', 'fsdp'))
- w_up: bfloat16 [1, 896, 4864], P(None, 'fsdp')
- w_lin: bfloat16 [1, 896, 4864], P(None, 'fsdp')
- w_down: bfloat16 [1, 4864, 896], P(None, 'fsdp')
Outputs:
- output 1: float32 [1, 896, 4864], P(None, 'fsdp')
- output 2: float32 [1, 896, 4864], P(None, 'fsdp')
- output 3: float32 [1, 4864, 896], P(None, 'fsdp')
- output 4: bfloat16 [131072, 896], P(('replica', 'fsdp'))
All inputs are finite; a program needn't handle non-finite values.
Results may differ from a plain program's by a relative error of at most 0.001.
Values are sent between devices in bfloat16 or wider.
A program may use at most 1 GiB of HBM per device.

v0:
```python
import jax
import jax.numpy as jnp
from jax import lax
from jax.sharding import PartitionSpec as P

NORM_EPS = 1e-5


def layer_grad(h_in, grad_acc, up_w, lin_w, down_w):
    h_f32 = h_in.astype(jnp.float32)
    inv_rms = lax.rsqrt(jnp.mean(h_f32 * h_f32, axis=-1, keepdims=True) + NORM_EPS)
    normed = h_f32 * inv_rms
    normed_b = normed.astype(jnp.bfloat16)
    pre_up = jnp.einsum('td,df->tf', normed_b, up_w, preferred_element_type=jnp.float32)
    pre_lin = jnp.einsum('td,df->tf', normed_b, lin_w, preferred_element_type=jnp.float32)
    up_sig = jax.nn.sigmoid(pre_up)
    up_act = pre_up * up_sig
    act_b = (up_act * pre_lin).astype(jnp.bfloat16)
    grad_b = grad_acc.astype(jnp.bfloat16)
    d_act = jnp.einsum('td,fd->tf', grad_b, down_w, preferred_element_type=jnp.float32)
    d_up = (d_act * pre_lin * up_sig * (1.0 + pre_up * (1.0 - up_sig))).astype(jnp.bfloat16)
    d_lin = (d_act * up_act).astype(jnp.bfloat16)
    g_down = jnp.einsum('tf,td->fd', act_b, grad_b, preferred_element_type=jnp.float32)
    g_up = jnp.einsum('td,tf->df', normed_b, d_up, preferred_element_type=jnp.float32)
    g_lin = jnp.einsum('td,tf->df', normed_b, d_lin, preferred_element_type=jnp.float32)
    d_norm = jnp.einsum('tf,df->td', d_up, up_w, preferred_element_type=jnp.float32) + jnp.einsum('tf,df->td', d_lin, lin_w, preferred_element_type=jnp.float32)
    d_h = inv_rms * (d_norm - normed * jnp.mean(d_norm * normed, axis=-1, keepdims=True))
    return grad_acc + d_h, g_up, g_lin, g_down


def reduce_shard(full_grad):
    own_rows = lax.psum_scatter(full_grad, 'fsdp', scatter_dimension=0, tiled=True)
    return lax.psum(own_rows, 'replica')


def solution(mesh):
    tok_spec = P(('replica', 'fsdp'), None)
    act_spec = P(None, ('replica', 'fsdp'), None)
    weight_spec = P(None, 'fsdp', None)

    def local_step(block_in, grad_out, w_up, w_lin, w_down):
        layers = block_in.shape[0]
        grad_acc = grad_out.astype(jnp.float32)
        up_list = []
        lin_list = []
        down_list = []
        for layer_idx in reversed(range(layers)):
            up_full = lax.all_gather(w_up[layer_idx], 'fsdp', axis=0, tiled=True)
            lin_full = lax.all_gather(w_lin[layer_idx], 'fsdp', axis=0, tiled=True)
            down_full = lax.all_gather(w_down[layer_idx], 'fsdp', axis=0, tiled=True)
            grad_acc, g_up, g_lin, g_down = layer_grad(block_in[layer_idx], grad_acc, up_full, lin_full, down_full)
            up_list.insert(0, reduce_shard(g_up))
            lin_list.insert(0, reduce_shard(g_lin))
            down_list.insert(0, reduce_shard(g_down))
        return jnp.stack(up_list), jnp.stack(lin_list), jnp.stack(down_list), grad_acc.astype(jnp.bfloat16)

    return jax.shard_map(local_step, mesh=mesh, in_specs=(act_spec, tok_spec, weight_spec, weight_spec, weight_spec), out_specs=(weight_spec, weight_spec, weight_spec, tok_spec), check_vma=False)
```

profile of v0, /device:TPU:1, one launch (start us, length us, event | category | flops | bytes accessed | tf_op | source)
XLA Modules:
  0.0 535.8 jit_solution(4479168002800993981)
XLA Ops:
  7.2 0.7 all-gather.9.cloned.1.call-update
  7.9 0.0 all-gather.11.cloned.1.call-start
  7.9 0.7 all-gather.11.cloned.1.call-update
  8.6 0.0 all-gather.7.cloned.1.call-start
  8.7 0.7 all-gather.7.cloned.1.call-update
  9.4 2.9 copy.9
  12.3 0.4 fusion.20
  12.8 25.1 %all-gather.9.cloned.1.call-done = bf16[1,896,4864]{2,1,0:T(8,128)(2,1)} async-done(((bf16[1,448,4864]{2,1,0:T(8,128)(2,1)}), bf16[1,896,4864]{2,1,0:T(8,128)(2,1)}) %all-gather.9.cloned.1.call-update) | async-done | bytes 8716304 | tf_op jit(solution)/shard_map/all_gather | solution.py:49
  37.9 17.3 %fusion.8 = f32[1024,4864]{1,0:T(8,128)} fusion(bf16[1,896,4864]{2,1,0:T(8,128)(2,1)} %all-gather.9.cloned.1.call-done, bf16[1,1024,896]{1,2,0:T(8,128)(2,1)S(1)} %copy.9, f32[1024]{0:T(1024)S(1)} %add_rsqrt_fusion), kind=kOutput, calls=%fused_computation.12 | convolution fusion | flops 8928231424 | bytes 30478336 | tf_op jit(solution)/shard_map/td,df->tf/dot_general | solution.py:15
  55.1 10.4 %all-gather.11.cloned.1.call-done = bf16[1,896,4864]{2,1,0:T(8,128)(2,1)} async-done(((bf16[1,448,4864]{2,1,0:T(8,128)(2,1)}), bf16[1,896,4864]{2,1,0:T(8,128)(2,1)}) %all-gather.11.cloned.1.call-update) | async-done | bytes 8716304 | tf_op jit(solution)/shard_map/all_gather | solution.py:48
  65.5 17.2 %fusion.4 = f32[1024,4864]{1,0:T(8,128)} fusion(bf16[1,896,4864]{2,1,0:T(8,128)(2,1)} %all-gather.11.cloned.1.call-done, bf16[1,1024,896]{1,2,0:T(8,128)(2,1)S(1)} %copy.9, f32[1024]{0:T(1024)S(1)} %add_rsqrt_fusion), kind=kOutput, calls=%fused_computation.8 | convolution fusion | flops 8928231424 | bytes 30478336 | tf_op jit(solution)/shard_map/td,df->tf/dot_general | solution.py:14
  82.7 10.4 %all-gather.7.cloned.1.call-done = bf16[1,4864,896]{2,1,0:T(8,128)(2,1)} async-done(((bf16[1,2432,896]{2,1,0:T(8,128)(2,1)}), bf16[1,4864,896]{2,1,0:T(8,128)(2,1)}) %all-gather.7.cloned.1.call-update) | async-done | bytes 8716304 | tf_op jit(solution)/shard_map/all_gather | solution.py:50
  93.2 28.8 %multiply_convert_fusion.1 = (bf16[1024,4864]{1,0:T(8,128)(2,1)}, bf16[1024,4864]{1,0:T(8,128)(2,1)}) fusion(f32[1024,4864]{1,0:T(8,128)} %fusion.4, f32[1024,4864]{1,0:T(8,128)} %fusion.8, bf16[1024,896]{1,0:T(8,128)(2,1)} %param.6, bf16[1,4864,896]{2,1,0:T(8,128)(2,1)} %all-gather.7.cloned.1.call-done), kind=kOutput, calls=%fused_computation.1 | convolution fusion | flops 8990228480 | bytes 70320128 | tf_op jit(solution)/shard_map/td,fd->tf/dot_general | solution.py:20
  122.0 15.6 %fusion.25 = f32[896,4864]{1,0:T(8,128)} fusion(bf16[1024,4864]{1,0:T(8,128)(2,1)} %get-tuple-element.11, bf16[1,1024,896]{1,2,0:T(8,128)(2,1)S(1)} %copy.9, f32[1024]{0:T(1024)S(1)} %add_rsqrt_fusion), kind=kOutput, calls=%fused_computation.28 | convolution fusion | flops 8928231424 | bytes 29233152 | tf_op jit(solution)/shard_map/td,tf->df/dot_general | solution.py:25
  137.6 0.0 reduce-scatter.4.cloned.1.call-start
  137.7 15.6 %fusion.27 = f32[896,4864]{1,0:T(8,128)} fusion(bf16[1024,4864]{1,0:T(8,128)(2,1)} %get-tuple-element.12, bf16[1,1024,896]{1,2,0:T(8,128)(2,1)S(1)} %copy.9, f32[1024]{0:T(1024)S(1)} %add_rsqrt_fusion), kind=kOutput, calls=%fused_computation.29 | convolution fusion | flops 8928231424 | bytes 29233152 | tf_op jit(solution)/shard_map/td,tf->df/dot_general | solution.py:24
  153.3 0.0 reduce-scatter.8.cloned.1.call-start
  153.3 24.6 %fusion.1 = f32[4864,896]{1,0:T(8,128)} fusion(bf16[1024,896]{1,0:T(8,128)(2,1)} %param.6, f32[1024,4864]{1,0:T(8,128)} %fusion.8, f32[1024,4864]{1,0:T(8,128)} %fusion.4), kind=kOutput, calls=%fused_computation.5 | convolution fusion | flops 8955363328 | bytes 59113472 | tf_op jit(solution)/shard_map/tf,td->fd/dot_general | solution.py:23
  177.9 0.0 all-reduce.3.cloned.1.call-start
  178.0 20.1 %reduce-scatter.4.cloned.1.call-done = f32[448,4864]{1,0:T(8,128)} async-done(((f32[896,4864]{1,0:T(8,128)}), f32[448,4864]{1,0:T(8,128)}) %reduce-scatter.4.cloned.1.call-update) | async-done | bytes 8716304 | tf_op jit(solution)/shard_map/reduce_scatter | solution.py:32
  198.1 31.3 %reduce-scatter.8.cloned.1.call-done = f32[2432,896]{1,0:T(8,128)} async-done(((f32[4864,896]{1,0:T(8,128)}), f32[2432,896]{1,0:T(8,128)}) %reduce-scatter.8.cloned.1.call-update) | async-done | bytes 8716304 | tf_op jit(solution)/shard_map/reduce_scatter | solution.py:32
  229.5 4.0 copy.10
  233.5 13.7 %fusion.2 = f32[1024,896]{0,1:T(8,128)S(1)} fusion(bf16[1024,4864]{1,0:T(8,128)(2,1)} %get-tuple-element.12, bf16[1,896,4864]{2,1,0:T(8,128)(2,1)} %all-gather.11.cloned.1.call-done), kind=kOutput, calls=%fused_computation.6 | convolution fusion | flops 8925478912 | bytes 22347776 | tf_op jit(solution)/shard_map/tf,df->td/dot_general | solution.py:26
  247.2 14.6 %fusion.15 = (f32[1024]{0:T(1024)S(1)}, f32[1024,896]{0,1:T(8,128)S(1)}) fusion(bf16[1,1024,896]{1,2,0:T(8,128)(2,1)S(1)} %copy.9, f32[1024]{0:T(1024)S(1)} %add_rsqrt_fusion, f32[1024,896]{0,1:T(8,128)S(1)} %fusion.2, bf16[1024,4864]{1,0:T(8,128)(2,1)} %get-tuple-element.11, bf16[1,896,4864]{2,1,0:T(8,128)(2,1)} %all-gather.9.cloned.1.call-done), kind=kOutput, calls=%fused_computation.21 | convolution fusion | flops 8930065408 | bytes 27860992 | tf_op jit(solution)/shard_map/tf,df->td/dot_general | solution.py:26
  261.8 2.4 fusion.19
  264.2 3.8 copy.11
  268.0 242.8 %all-reduce.3.cloned.1.call-done = (f32[1,448,4864]{2,1,0:T(8,128)}, f32[1,448,4864]{2,1,0:T(8,128)}, f32[1,2432,896]{2,1,0:T(8,128)}) async-done(((f32[1,448,4864]{2,1,0:T(8,128)}, f32[1,448,4864]{2,1,0:T(8,128)}, f32[1,2432,896]{2,1,0:T(8,128)}), (f32[1,448,4864]{2,1,0:T(8,128)}, f32[1,448,4864]{2,1,0:T(8,128)}, f32[1,2432,896]{2,1,0:T(8,128)})) %all-reduce.3.cloned.1.call-update) | async-done | bytes 26148880 | tf_op jit(solution)/shard_map/psum | solution.py:33
  510.8 8.6 %copy.15 = f32[1,448,4864]{2,1,0:T(8,128)} copy(f32[1,448,4864]{2,1,0:T(8,128)} %get-tuple-element.15) | data formatting | bytes 17432576
  519.4 4.4 copy.16
  523.8 1.6 slice-done.1
  525.4 0.1 slice-done.2
  525.5 3.5 copy.17
  (18 shorter events, 0.2 us)
Async XLA Ops:
  7.2 30.7 %all-gather.9.cloned.1.call-start = ((), (), s32[]{:S(2)}) async-start(), calls=%async_computation.7 | async-start | bytes 13074432 | tf_op jit(solution)/shard_map/all_gather | solution.py:49
  7.9 57.6 %all-gather.11.cloned.1.call-start = ((), (), s32[]{:S(2)}) async-start(), calls=%async_computation.8 | async-start | bytes 13074432 | tf_op jit(solution)/shard_map/all_gather | solution.py:48
  8.6 84.5 %all-gather.7.cloned.1.call-start = ((), (), s32[]{:S(2)}) async-start(), calls=%async_computation.6 | async-start | bytes 13074432 | tf_op jit(solution)/shard_map/all_gather | solution.py:50
  9.4 168.6 %reduce-scatter.6.cloned.1.call-start = ((), (), s32[]{:S(2)}) async-start(), calls=%async_computation.4 | async-start | bytes 26148864 | tf_op jit(solution)/shard_map/reduce_scatter | solution.py:32
  137.6 60.5 %reduce-scatter.4.cloned.1.call-start = ((), (), s32[]{:S(2)}) async-start(), calls=%async_computation.3 | async-start | bytes 26148864 | tf_op jit(solution)/shard_map/reduce_scatter | solution.py:32
  153.3 76.1 %reduce-scatter.8.cloned.1.call-start = ((), (), s32[]{:S(2)}) async-start(), calls=%async_computation.5 | async-start | bytes 26148864 | tf_op jit(solution)/shard_map/reduce_scatter | solution.py:32
  177.9 332.8 %all-reduce.3.cloned.1.call-start = ((), (), s32[]{:S(2)}) async-start(), calls=%async_computation.9 | async-start | bytes 52297728 | tf_op jit(solution)/shard_map/psum | solution.py:33
  247.2 14.6 %copy-start.1 = (bf16[1024,896]{0,1:T(8,128)(2,1)S(1)}, bf16[1024,896]{0,1:T(8,128)(2,1)}, u32[]{:S(2)}) copy-start(bf16[1024,896]{0,1:T(8,128)(2,1)} %copy.10) | copy-start | bytes 5505028
  510.8 8.6 %copy-start = (f32[1,448,4864]{2,1,0:T(8,128)S(1)}, f32[1,448,4864]{2,1,0:T(8,128)}, u32[]{:S(2)}) copy-start(f32[1,448,4864]{2,1,0:T(8,128)} %get-tuple-element.16) | copy-start | bytes 26148868
  510.8 13.0 %slice-start = ((s8[8716288]{0:T(1024)(128)(4,1)}), s8[4194304]{0:T(1024)(128)(4,1)S(1)}, s32[]{:S(2)}) async-start(s8[8716288]{0:T(1024)(128)(4,1)} %bitcast.41), calls=%async_computation.10 | async-start | bytes 8388608
  510.8 14.6 %slice-start.1 = ((s8[8716288]{0:T(1024)(128)(4,1)}), s8[4194304]{0:T(1024)(128)(4,1)S(1)}, s32[]{:S(2)}) async-start(s8[8716288]{0:T(1024)(128)(4,1)} %bitcast.41), calls=%async_computation.11 | async-start | bytes 8388608
  519.4 6.1 %slice-start.2 = ((s8[8716288]{0:T(1024)(128)(4,1)}), s8[327680]{0:T(1024)(128)(4,1)S(1)}, s32[]{:S(2)}) async-start(s8[8716288]{0:T(1024)(128)(4,1)} %bitcast.41), calls=%async_computation.12 | async-start | bytes 655360
Sparse Core Ops, SparseCore 0:
  9.6 28.2 all-gather.8
  39.6 25.9 all-gather.10
  67.2 25.9 all-gather.6
  137.7 29.0 reduce-scatter.5
  169.1 28.9 reduce-scatter.3
  200.4 28.9 reduce-scatter.7
  235.7 274.9 all-reduce.2
where the time goes:
time: 537 us; the launch traced here: 536 us
  waiting for transfers between devices  342 us (64%)
  matrix products  147 us (27%)
  local copies, waits for them, and re-layouts  29 us (5%)
  between operations  14.2 us (3%)
    psum x1, waiting for transfers between devices, reduce_shard(): return lax.psum(own_rows, 'replica')  243 us
    reduce_scatter x3, waiting for transfers between devices, reduce_shard(): lax.psum_scatter(full_grad, 'fsdp', scatter_dimension=0, tiled=True)  51.4 us
    unnamed x16, local copies, waits for them, and re-layouts  29 us
    dot_general x1, matrix products, layer_grad(): jnp.einsum('td,fd->tf', grad_b, down_w, preferred_element_type=jnp.float32)  28.8 us
    all_gather x1, waiting for transfers between devices, local_step(): lin_full = lax.all_gather(w_lin[layer_idx], 'fsdp', axis=0, tiled=True)  25.1 us
    dot_general x1, matrix products, layer_grad(): jnp.einsum('tf,td->fd', act_b, grad_b, preferred_element_type=jnp.float32)  24.6 us
    dot_general x1, matrix products, layer_grad(): jnp.einsum('td,df->tf', normed_b, lin_w, preferred_element_type=jnp.float32)  17.3 us
    dot_general x1, matrix products, layer_grad(): jnp.einsum('td,df->tf', normed_b, up_w, preferred_element_type=jnp.float32)  17.2 us
  transfers between devices with their start and end apart: 7, of which 6 were waited for; matrix products, arithmetic and copies ran while one was open for 22% of the time, Pallas kernels for 0%

commit v1 on v0

v1 whole, which is shorter than its diff:
```python
import jax
import jax.numpy as jnp
from jax import lax
from jax.experimental import pallas as pl
from jax.experimental.pallas import tpu as pltpu
from jax.sharding import PartitionSpec as P

NORM_EPS = 1e-5
MESH = pl.DeviceIdType.MESH
F32 = jnp.float32
BF16 = jnp.bfloat16

D = 896
TOK = 1024
FF = 4864
HALF = FF // 2
SLAB = 128
N_SLAB = HALF // SLAB
CHUNK = 256
N_CHUNK = -(-HALF // CHUNK)
LAST = HALF - (N_CHUNK - 1) * CHUNK
ROWS = D // 2
TILE = 256
BLK = (224, 56, 16)
HALVES = (((0, 112), (112, 112)), ((0, 32), (32, 24)), ((0, 8), (8, 8)))
N_STAGE = 14


def dot(a, b, dims):
    return lax.dot_general(a, b, (dims, ((), ())), preferred_element_type=F32)


def kernel(h_ref, g_ref, w1_ref, w3_ref, w2_ref,
           o1_ref, o3_ref, o2_ref, oh_ref, wx_ref, dnx_ref,
           slab, l3, l3g, ra0, rb0, ra1, rb1, ra2, rb2,
           n_v, nt_v, gb_v, gt_v, dn_v, a_v, du_v, dv_v, w1_v, w3_v, w2_v, tb_v, dnr_v, hr_v, oh_v,
           send_sem, recv_sem, out_sem, xs_sem, xr_sem, w_sem, ws_sem, wr_sem, in_sem, is_sem, ir_sem, fin_sem):
    rep = lax.axis_index("replica")
    core = lax.axis_index("fsdp")
    coord = (lax.rem(rep, 4), lax.rem(lax.div(rep, 4), 4), lax.div(rep, 16))
    stride = (1, 4, 16)
    right = []
    left = []
    for d in range(3):
        right.append((rep + stride[d] * (lax.rem(coord[d] + 1, 4) - coord[d]), core))
        left.append((rep + stride[d] * (lax.rem(coord[d] + 3, 4) - coord[d]), core))
    peer = (rep, 1 - core)
    ra = (ra0, ra1, ra2)
    rb = (rb0, rb1, rb2)

    def rows(level, s, c, block, off, size, gather=False):
        base = block * BLK[level] + off
        if level == 1:
            base = base + coord[c] * BLK[0]
        ref = slab if level < 2 else (l3g if gather else l3)
        return ref.at[s, c, pl.ds(pl.multiple_of(base, 8), size), :]

    def copies(q, s, c):
        par = lax.rem(s, 2)
        if q < 6:
            level, second, gather = q // 2, q % 2, False
        else:
            level, second, gather = 2 - (q - 6) // 2, q % 2, True
        d = (c + level) % 3
        i = coord[d]
        blk = BLK[level]
        (f0, fn), (s0, sn) = HALVES[level]
        if not gather:
            if second == 0:
                b = lax.rem(i + 2, 4)
                pairs = ((rows(level, s, c, b, f0, fn), ra[level].at[par, c, 0, pl.ds(0, fn), :]),
                         (rows(level, s, c, b, s0, sn), ra[level].at[par, c, 1, pl.ds(0, sn), :]))
            else:
                pairs = ((rows(level, s, c, lax.rem(i + 1, 4), 0, blk), rb[level].at[par, c, 0]),
                         (rows(level, s, c, lax.rem(i + 3, 4), 0, blk), rb[level].at[par, c, 1]))
        else:
            if second == 0:
                own = rows(level, s, c, i, 0, blk, True)
                pairs = ((own, own), (own, own))
            else:
                to_right = rows(level, s, c, lax.rem(i + 3, 4), s0, sn, True)
                to_left = rows(level, s, c, lax.rem(i + 1, 4), f0, fn, True)
                pairs = ((to_right, to_right), (to_left, to_left))
        out = []
        for way, (src, dst) in enumerate(pairs):
            out.append(pltpu.make_async_remote_copy(
                src_ref=src, dst_ref=dst,
                send_sem=send_sem.at[par, q, 2 * c + way], recv_sem=recv_sem.at[par, q, 2 * c + way],
                device_id=(right[d], left[d])[way], device_id_type=MESH))
        return out

    def send(q, s):
        for c in range(3):
            for cp in copies(q, s, c):
                cp.start()

    def wait(q, s):
        for c in range(3):
            for cp in copies(q, s, c):
                cp.wait()

    def add_first(level, s):
        par = lax.rem(s, 2)
        (f0, fn), (s0, sn) = HALVES[level]
        for c in range(3):
            i = coord[(c + level) % 3]
            one = rows(level, s, c, lax.rem(i + 1, 4), f0, fn)
            one[...] = one[...] + ra[level][par, c, 0, 0:fn, :]
            two = rows(level, s, c, lax.rem(i + 3, 4), s0, sn)
            two[...] = two[...] + ra[level][par, c, 1, 0:sn, :]

    def add_second(level, s):
        par = lax.rem(s, 2)
        for c in range(3):
            i = coord[(c + level) % 3]
            own = rows(level, s, c, i, 0, BLK[level])
            total = own[...] + rb[level][par, c, 0] + rb[level][par, c, 1]
            if level == 1:
                l3[s, c, 0:56, :] = total
                l3[s, c, 56:64, :] = jnp.zeros((8, SLAB), F32)
            else:
                rows(level, s, c, i, 0, BLK[level], True)[...] = total

    def out_copies(s):
        par = lax.rem(s, 2)
        cols = pl.ds(pl.multiple_of(core * HALF + s * SLAB, 128), SLAB)
        mine = pl.ds(pl.multiple_of(core * ROWS, 8), ROWS)
        theirs = pl.ds(pl.multiple_of((1 - core) * ROWS, 8), ROWS)
        local, remote = [], []
        for c, o_ref in ((0, o1_ref), (1, o3_ref)):
            local.append(pltpu.make_async_copy(slab.at[s, c, mine, :], o_ref.at[:, cols], out_sem.at[par, c]))
            remote.append(pltpu.make_async_remote_copy(
                src_ref=slab.at[s, c, theirs, :], dst_ref=o_ref.at[:, cols],
                send_sem=xs_sem.at[par, c], recv_sem=xr_sem.at[par, c], device_id=peer, device_id_type=MESH))
        local.append(pltpu.make_async_copy(
            tb_v.at[par], o2_ref.at[pl.ds(pl.multiple_of(s * SLAB, 128), SLAB), :], out_sem.at[par, 2]))
        return local, remote

    def stage(j, s):
        if j == 13:
            local, remote = out_copies(s)
            for cp in local + remote:
                cp.wait()
            return
        if j > 0:
            wait(j - 1, s)
        if j in (1, 3, 5):
            add_first(j // 2, s)
        if j in (2, 4, 6):
            add_second(j // 2 - 1, s)
        if j == 8:
            for c in range(3):
                own = rows(1, s, c, coord[(c + 1) % 3], 0, BLK[1])
                own[...] = l3g[s, c, 0:56, :]
        if j < 12:
            send(j, s)
        else:
            tb_v[lax.rem(s, 2)] = slab[s, 2].T
            local, remote = out_copies(s)
            for cp in remote + local:
                cp.start()

    def w_copies(k, size):
        off = pl.multiple_of(k * CHUNK, 128)
        at = pl.multiple_of(core * HALF + k * CHUNK, 128)
        mine = pl.ds(pl.multiple_of(core * ROWS, 16), ROWS)
        theirs = pl.ds(pl.multiple_of((1 - core) * ROWS, 16), ROWS)
        return [
            pltpu.make_async_copy(w1_ref.at[:, pl.ds(at, size)], w1_v.at[mine, pl.ds(0, size)], w_sem.at[0]),
            pltpu.make_async_copy(w3_ref.at[:, pl.ds(at, size)], w3_v.at[mine, pl.ds(0, size)], w_sem.at[1]),
            pltpu.make_async_copy(w2_ref.at[pl.ds(off, size), :], w2_v.at[pl.ds(0, size), :], w_sem.at[2]),
            pltpu.make_async_copy(wx_ref.at[0, :, pl.ds(off, size)], w1_v.at[theirs, pl.ds(0, size)], w_sem.at[3]),
            pltpu.make_async_copy(wx_ref.at[1, :, pl.ds(off, size)], w3_v.at[theirs, pl.ds(0, size)], w_sem.at[4]),
        ]

    def x_copies(k, size):
        off = pl.multiple_of(k * CHUNK, 128)
        at = pl.multiple_of((1 - core) * HALF + k * CHUNK, 128)
        return [pltpu.make_async_remote_copy(
            src_ref=w_ref.at[:, pl.ds(at, size)], dst_ref=wx_ref.at[m, :, pl.ds(off, size)],
            send_sem=ws_sem.at[k, m], recv_sem=wr_sem.at[k, m], device_id=peer, device_id_type=MESH)
            for m, w_ref in ((0, w1_ref), (1, w3_ref))]

    own_tok = pl.ds(pl.multiple_of(core * TOK, TOK), TOK)
    own_h = pltpu.make_async_copy(h_ref, n_v.at[own_tok, :], in_sem.at[0])
    own_g = pltpu.make_async_copy(g_ref, gb_v.at[own_tok, :], in_sem.at[1])
    own_h.start()
    own_g.start()

    barrier = pltpu.get_barrier_semaphore()
    for dev in right + left + [peer]:
        pl.semaphore_signal(barrier, inc=1, device_id=dev, device_id_type=MESH)
    pl.semaphore_wait(barrier, 7)

    peer_h = pltpu.make_async_remote_copy(
        src_ref=h_ref, dst_ref=n_v.at[own_tok, :], send_sem=is_sem.at[0], recv_sem=ir_sem.at[0],
        device_id=peer, device_id_type=MESH)
    peer_g = pltpu.make_async_remote_copy(
        src_ref=g_ref, dst_ref=gb_v.at[own_tok, :], send_sem=is_sem.at[1], recv_sem=ir_sem.at[1],
        device_id=peer, device_id_type=MESH)
    peer_h.start()
    for cp in x_copies(0, CHUNK):
        cp.start()
    peer_g.start()

    def push(k, _):
        for cp in x_copies(k, CHUNK):
            cp.start()
        return 0

    lax.fori_loop(1, N_CHUNK - 1, push, 0)
    for cp in x_copies(N_CHUNK - 1, LAST):
        cp.start()

    def zero(m, _):
        dn_v[pl.ds(pl.multiple_of(m * 64, 64), 64), :] = jnp.zeros((64, D), F32)
        return 0

    lax.fori_loop(0, 2 * TOK // 64, zero, 0)

    def norm(base):
        def body(m, _):
            at = pl.multiple_of(base + m * 128, 128)
            hf = n_v[pl.ds(at, 128), :].astype(F32)
            inv = lax.rsqrt(jnp.mean(hf * hf, axis=-1, keepdims=True) + NORM_EPS)
            nb = (hf * inv).astype(BF16)
            n_v[pl.ds(at, 128), :] = nb
            nt_v[:, pl.ds(at, 128)] = nb.T
            return 0
        lax.fori_loop(0, TOK // 128, body, 0)

    def flip(base):
        def body(m, _):
            at = pl.multiple_of(base + m * 128, 128)
            gt_v[:, pl.ds(at, 128)] = gb_v[pl.ds(at, 128), :].T
            return 0
        lax.fori_loop(0, TOK // 128, body, 0)

    def w_fetch(k):
        @pl.when(k < N_CHUNK - 1)
        def _():
            for cp in x_copies(k, CHUNK):
                cp.wait()
            for cp in w_copies(k, CHUNK):
                cp.start()

        @pl.when(k == N_CHUNK - 1)
        def _():
            for cp in x_copies(k, LAST):
                cp.wait()
            for cp in w_copies(k, LAST):
                cp.start()
            w1_v[:, LAST:] = jnp.zeros((D, CHUNK - LAST), BF16)
            w3_v[:, LAST:] = jnp.zeros((D, CHUNK - LAST), BF16)
            w2_v[LAST:, :] = jnp.zeros((CHUNK - LAST, D), BF16)

    own_h.wait()
    norm(core * TOK)
    own_g.wait()
    flip(core * TOK)
    w_fetch(0)
    peer_h.wait()
    norm((1 - core) * TOK)
    peer_g.wait()
    flip((1 - core) * TOK)

    def phase_a(k):
        @pl.when(k < N_CHUNK - 1)
        def _():
            for cp in w_copies(k, CHUNK):
                cp.wait()

        @pl.when(k == N_CHUNK - 1)
        def _():
            for cp in w_copies(k, LAST):
                cp.wait()

        def body(m, _):
            at = pl.ds(pl.multiple_of(m * TILE, TILE), TILE)
            nb = n_v[at, :]
            pre_up = dot(nb, w1_v[...], ((1,), (0,)))
            pre_lin = dot(nb, w3_v[...], ((1,), (0,)))
            d_act = dot(gb_v[at, :], w2_v[...], ((1,), (1,)))
            sig = jax.nn.sigmoid(pre_up)
            up_act = pre_up * sig
            a_v[at, :] = (up_act * pre_lin).astype(BF16)
            d_up = (d_act * pre_lin * sig * (1.0 + pre_up * (1.0 - sig))).astype(BF16)
            d_lin = (d_act * up_act).astype(BF16)
            du_v[at, :] = d_up
            dv_v[at, :] = d_lin
            dn_v[at, :] += dot(d_up, w1_v[...], ((1,), (1,))) + dot(d_lin, w3_v[...], ((1,), (1,)))
            return 0

        lax.fori_loop(0, 2 * TOK // TILE, body, 0)

        @pl.when(k < N_CHUNK - 1)
        def _():
            w_fetch(k + 1)

    def phase_b(k):
        s0 = 2 * k
        s1 = 2 * k + 1 - lax.div(k, N_CHUNK - 1)

        def body(m, _):
            at = pl.ds(pl.multiple_of(m * 128, 128), 128)
            for c, (lhs, rhs) in enumerate(((nt_v, du_v), (nt_v, dv_v), (gt_v, a_v))):
                out = dot(lhs[at, :], rhs[...], ((1,), (0,)))
                slab[s1, c, at, :] = out[:, SLAB:]
                slab[s0, c, at, :] = out[:, :SLAB]
            return 0

        lax.fori_loop(0, D // 128, body, 0)

    dn_copy = pltpu.make_async_remote_copy(
        src_ref=dn_v.at[pl.ds(pl.multiple_of((1 - core) * TOK, TOK), TOK), :], dst_ref=dnx_ref,
        send_sem=is_sem.at[2], recv_sem=ir_sem.at[2], device_id=peer, device_id_type=MESH)

    def final(m):
        at = pl.ds(pl.multiple_of(m * TILE, TILE), TILE)
        in1 = pltpu.make_async_copy(dnx_ref.at[at, :], dnr_v, fin_sem.at[0])
        in2 = pltpu.make_async_copy(h_ref.at[at, :], hr_v, fin_sem.at[1])
        in1.start()
        in2.start()
        in1.wait()
        in2.wait()
        mine = pl.multiple_of(core * TOK + m * TILE, TILE)

        def body(p, _):
            sub = pl.ds(pl.multiple_of(p * 64, 64), 64)
            here = pl.ds(pl.multiple_of(mine + p * 64, 64), 64)
            hf = hr_v[sub, :].astype(F32)
            inv = lax.rsqrt(jnp.mean(hf * hf, axis=-1, keepdims=True) + NORM_EPS)
            y = hf * inv
            d_norm = dn_v[here, :] + dnr_v[sub, :]
            d_h = inv * (d_norm - y * jnp.mean(d_norm * y, axis=-1, keepdims=True))
            oh_v[sub, :] = (gb_v[here, :].astype(F32) + d_h).astype(BF16)
            return 0

        lax.fori_loop(0, TILE // 64, body, 0)
        out = pltpu.make_async_copy(oh_v, oh_ref.at[at, :], fin_sem.at[2])
        out.start()
        out.wait()

    def step(tt, _):
        k = lax.div(tt, 2)
        odd = lax.rem(tt, 2)

        @pl.when((odd == 0) & (k < N_CHUNK))
        def _():
            phase_a(k)

        @pl.when((odd == 1) & (k < N_CHUNK))
        def _():
            phase_b(k)

        @pl.when(tt == 2 * N_CHUNK - 1)
        def _():
            dn_copy.start()

        @pl.when(tt == 2 * N_CHUNK + 2)
        def _():
            dn_copy.wait()

        @pl.when((tt >= 2 * N_CHUNK + 2) & (tt < 2 * N_CHUNK + 2 + TOK // TILE))
        def _():
            final(tt - (2 * N_CHUNK + 2))

        for j in reversed(range(N_STAGE)):
            s = tt - 1 - j

            @pl.when((s >= 0) & (s < N_SLAB))
            def _(j=j, s=s):
                stage(j, s)

        return 0

    lax.fori_loop(0, N_SLAB + N_STAGE, step, 0)


def solution(mesh):
    tok_spec = P(('replica', 'fsdp'), None)
    act_spec = P(None, ('replica', 'fsdp'), None)
    weight_spec = P(None, 'fsdp', None)

    def local_step(block_in, grad_out, w_up, w_lin, w_down):
        any_spec = pl.BlockSpec(memory_space=pl.ANY)
        dma = pltpu.SemaphoreType.DMA
        o1, o3, o2, oh, _, _ = pl.pallas_call(
            kernel,
            out_shape=(
                jax.ShapeDtypeStruct((ROWS, FF), F32),
                jax.ShapeDtypeStruct((ROWS, FF), F32),
                jax.ShapeDtypeStruct((HALF, D), F32),
                jax.ShapeDtypeStruct((TOK, D), BF16),
                jax.ShapeDtypeStruct((2, ROWS, HALF), BF16),
                jax.ShapeDtypeStruct((TOK, D), F32),
            ),
            in_specs=[any_spec] * 5,
            out_specs=(any_spec,) * 6,
            scratch_shapes=[
                pltpu.VMEM((N_SLAB, 3, D, SLAB), F32),
                pltpu.VMEM((N_SLAB, 3, 64, SLAB), F32),
                pltpu.VMEM((N_SLAB, 3, 64, SLAB), F32),
                pltpu.VMEM((2, 3, 2, 112, SLAB), F32),
                pltpu.VMEM((2, 3, 2, 224, SLAB), F32),
                pltpu.VMEM((2, 3, 2, 32, SLAB), F32),
                pltpu.VMEM((2, 3, 2, 56, SLAB), F32),
                pltpu.VMEM((2, 3, 2, 8, SLAB), F32),
                pltpu.VMEM((2, 3, 2, 16, SLAB), F32),
                pltpu.VMEM((2 * TOK, D), BF16),
                pltpu.VMEM((D, 2 * TOK), BF16),
                pltpu.VMEM((2 * TOK, D), BF16),
                pltpu.VMEM((D, 2 * TOK), BF16),
                pltpu.VMEM((2 * TOK, D), F32),
                pltpu.VMEM((2 * TOK, CHUNK), BF16),
                pltpu.VMEM((2 * TOK, CHUNK), BF16),
                pltpu.VMEM((2 * TOK, CHUNK), BF16),
                pltpu.VMEM((D, CHUNK), BF16),
                pltpu.VMEM((D, CHUNK), BF16),
                pltpu.VMEM((CHUNK, D), BF16),
                pltpu.VMEM((2, SLAB, D), F32),
                pltpu.VMEM((TILE, D), F32),
                pltpu.VMEM((TILE, D), BF16),
                pltpu.VMEM((TILE, D), BF16),
                dma((2, 12, 6)),
                dma((2, 12, 6)),
                dma((2, 3)),
                dma((2, 2)),
                dma((2, 2)),
                dma((5,)),
                dma((N_CHUNK, 2)),
                dma((N_CHUNK, 2)),
                dma((2,)),
                dma((3,)),
                dma((3,)),
                dma((3,)),
            ],
            compiler_params=pltpu.CompilerParams(
                collective_id=0, has_side_effects=True, vmem_limit_bytes=67043328),
        )(block_in[0], grad_out, w_up[0], w_lin[0], w_down[0])
        return o1[None], o3[None], o2[None], oh

    return jax.shard_map(local_step, mesh=mesh, in_specs=(act_spec, tok_spec, weight_spec, weight_spec, weight_spec), out_specs=(weight_spec, weight_spec, weight_spec, tok_spec), check_vma=False)
```

time: 537 us -> 309 us (0.58)
  waiting for transfers between devices: 342 us -> 0 us
  Pallas kernels: 0 us -> 289 us
  matrix products: 147 us -> 0 us
  between operations: 14.2 us -> 0.67 us
  local copies, waits for them, and re-layouts: 29 us -> 19.5 us
    pallas_call x0 -> x1, Pallas kernels: none -> 289 us  [local_step(): pl.pallas_call(kernel, out_shape=(jax.ShapeDtypeStruct((ROWS, FF), F32),...]
    psum x1 -> x0, waiting for transfers between devices: 243 us -> none  [reduce_shard(): return lax.psum(own_rows, 'replica')]
    dot_general x8 -> x0, matrix products: 147 us -> none  [the longest x1 28.8 us: layer_grad(): jnp.einsum('td,fd->tf', grad_b, down_w, preferred_element_type=jnp.float32)]
    reduce_scatter x3 -> x0, waiting for transfers between devices: 51.4 us -> none  [reduce_shard(): lax.psum_scatter(full_grad, 'fsdp', scatter_dimension=0, tiled=True)]
    all_gather x3 -> x0, waiting for transfers between devices: 45.9 us -> none  [the longest x1 25.1 us: local_step(): lin_full = lax.all_gather(w_lin[layer_idx], 'fsdp', axis=0, tiled=True)]
    unnamed x16 -> x14, local copies, waits for them, and re-layouts: 29 us -> 19.5 us
  transfers between devices with their start and end apart: 7 -> 0, of which waited for: 6 -> 0; matrix products, arithmetic and copies ran while one was open for 22% -> 0% of each run, Pallas kernels for 0% -> 0%
where the time goes in v1:
time: 309 us
  Pallas kernels  289 us (94%)
  local copies, waits for them, and re-layouts  19.5 us (6%)
    pallas_call x1, Pallas kernels, local_step(): pl.pallas_call(kernel, out_shape=(jax.ShapeDtypeStruct((ROWS, FF), F32),...  289 us
    unnamed x14, local copies, waits for them, and re-layouts  19.5 us

profile of v1, /device:TPU:1, one launch (start us, length us, event | category | flops | bytes accessed | tf_op | source)
XLA Modules:
  0.0 308.8 jit_solution(3252358537162135423)
XLA Ops:
  0.6 288.7 %shard_map.84 = (f32[448,4864]{1,0:T(8,128)}, f32[448,4864]{1,0:T(8,128)}, f32[2432,896]{1,0:T(8,128)}, bf16[1024,896]{1,0:T(8,128)(2,1)}, bf16[2,448,2432]{2,1,0:T(8,128)(2,1)}, /*index=5*/f32[1024,896]{1,0:T(8,128)}) custom-call(bf16[1024,896]{1,0:T(8,128)(2,1)} %bitcast.15, bf16[1024,896]{1,0:T(8,128)(2,1)} %g_ref.1, bf16[448,4864]{1,0:T(8,128)(2,1)} %bitcast.12, ...), custom_call_target="tpu_custom_call" | custom-call | tf_op jit(solution)/shard_map/pallas_call | solution.py:388
  289.3 0.0 copy-start
  289.3 0.0 slice-start
  289.3 0.0 slice-start.1
  289.3 8.6 %copy.13 = f32[1,448,4864]{2,1,0:T(8,128)} copy(f32[1,448,4864]{2,1,0:T(8,128)} %bitcast.11) | data formatting | bytes 17432576
  298.0 0.0 copy-done
  298.0 0.0 slice-start.2
  298.0 4.4 %copy.14 = f32[1,448,4864]{2,1,0:T(8,128)} copy(f32[1,448,4864]{2,1,0:T(8,128)S(1)} %bitcast.10) | data formatting | bytes 17432576
  302.4 0.0 slice-done
  302.4 1.6 slice-done.1
  304.0 0.1 slice-done.2
  304.0 0.0 copy-start.1
  304.0 3.5 %copy.15 = f32[1,2432,896]{2,1,0:T(8,128)} copy(f32[1,2432,896]{2,1,0:T(8,128)S(1)} %bitcast.9) | data formatting | bytes 17432576
  307.6 0.0 copy-done.1
  307.6 1.2 copy.16
  (1 shorter events, 0.0 us)
Async XLA Ops:
  289.3 8.6 %copy-start = (f32[448,4864]{1,0:T(8,128)S(1)}, f32[448,4864]{1,0:T(8,128)}, u32[]{:S(2)}) copy-start(f32[448,4864]{1,0:T(8,128)} %get-tuple-element.9) | copy-start | bytes 26148868
  289.3 13.1 %slice-start = ((s8[8716288]{0:T(1024)(128)(4,1)}), s8[4194304]{0:T(1024)(128)(4,1)S(1)}, s32[]{:S(2)}) async-start(s8[8716288]{0:T(1024)(128)(4,1)} %bitcast.7), calls=%async_computation | async-start | bytes 8388608
  289.3 14.6 %slice-start.1 = ((s8[8716288]{0:T(1024)(128)(4,1)}), s8[4194304]{0:T(1024)(128)(4,1)S(1)}, s32[]{:S(2)}) async-start(s8[8716288]{0:T(1024)(128)(4,1)} %bitcast.7), calls=%async_computation.1 | async-start | bytes 8388608
  298.0 6.1 %slice-start.2 = ((s8[8716288]{0:T(1024)(128)(4,1)}), s8[327680]{0:T(1024)(128)(4,1)S(1)}, s32[]{:S(2)}) async-start(s8[8716288]{0:T(1024)(128)(4,1)} %bitcast.7), calls=%async_computation.2 | async-start | bytes 655360
  304.0 3.5 %copy-start.1 = (bf16[1024,896]{1,0:T(8,128)(2,1)S(1)}, bf16[1024,896]{1,0:T(8,128)(2,1)}, u32[]{:S(2)}) copy-start(bf16[1024,896]{1,0:T(8,128)(2,1)} %get-tuple-element.19) | copy-start | bytes 5505028

commit v2 on v1

v2 whole, which is shorter than its diff:
```python
import jax
import jax.numpy as jnp
from jax import lax
from jax.experimental import pallas as pl
from jax.experimental.pallas import tpu as pltpu
from jax.sharding import PartitionSpec as P

NORM_EPS = 1e-5
MESH = pl.DeviceIdType.MESH
F32 = jnp.float32
BF16 = jnp.bfloat16

D = 896
TOK = 1024
FF = 4864
HALF = FF // 2
SLAB = 128
N_SLAB = HALF // SLAB
CHUNK = 256
N_CHUNK = -(-HALF // CHUNK)
LAST = HALF - (N_CHUNK - 1) * CHUNK
ROWS = D // 2
TILE = 128
TILE_1 = 512
TILE_2 = 1024
TILE_B = 128
BLK = (224, 56, 16)
HALVES = (((0, 112), (112, 112)), ((0, 32), (32, 24)), ((0, 8), (8, 8)))
N_STAGE = 14
FIN = 2 * N_CHUNK + 4


def dot(a, b, dims):
    return lax.dot_general(a, b, (dims, ((), ())), preferred_element_type=F32)


def kernel(h_ref, g_ref, w1_ref, w3_ref, w2_ref,
           slab, oh_ref, wx_ref, dnx_ref,
           l3, l3g, ra0, rb0, ra1, rb1, ra2, rb2,
           n_v, nt_v, gb_v, gt_v, dn_v, a_v, du_v, dv_v, w1_v, w3_v, w2_v, xb, dnr_v, hr_v,
           send_sem, recv_sem, xs_sem, xr_sem, w_sem, ws_sem, wr_sem, in_sem, is_sem, ir_sem, fin_sem):
    rep = lax.axis_index("replica")
    core = lax.axis_index("fsdp")
    coord = (lax.rem(rep, 4), lax.rem(lax.div(rep, 4), 4), lax.div(rep, 16))
    stride = (1, 4, 16)
    right = []
    left = []
    for d in range(3):
        right.append((rep + stride[d] * (lax.rem(coord[d] + 1, 4) - coord[d]), core))
        left.append((rep + stride[d] * (lax.rem(coord[d] + 3, 4) - coord[d]), core))
    peer = (rep, 1 - core)
    ra = (ra0, ra1, ra2)
    rb = (rb0, rb1, rb2)

    def rows(level, s, c, block, off, size, gather=False):
        base = block * BLK[level] + off
        if level == 1:
            base = base + coord[c] * BLK[0]
        ref = slab if level < 2 else (l3g if gather else l3)
        if level == 2:
            s = lax.rem(s, 3 if gather else 2)
        return ref.at[s, c, pl.ds(pl.multiple_of(base, 8), size), :]

    def copies(q, s, c):
        par = lax.rem(s, 2)
        if q < 6:
            level, second, gather = q // 2, q % 2, False
        else:
            level, second, gather = 2 - (q - 6) // 2, q % 2, True
        d = (c + level) % 3
        i = coord[d]
        blk = BLK[level]
        (f0, fn), (s0, sn) = HALVES[level]
        if not gather:
            if second == 0:
                b = lax.rem(i + 2, 4)
                pairs = ((rows(level, s, c, b, f0, fn), ra[level].at[par, c, 0, pl.ds(0, fn), :]),
                         (rows(level, s, c, b, s0, sn), ra[level].at[par, c, 1, pl.ds(0, sn), :]))
            else:
                pairs = ((rows(level, s, c, lax.rem(i + 1, 4), 0, blk), rb[level].at[par, c, 0]),
                         (rows(level, s, c, lax.rem(i + 3, 4), 0, blk), rb[level].at[par, c, 1]))
        else:
            if second == 0:
                own = rows(level, s, c, i, 0, blk, True)
                pairs = ((own, own), (own, own))
            else:
                to_right = rows(level, s, c, lax.rem(i + 3, 4), s0, sn, True)
                to_left = rows(level, s, c, lax.rem(i + 1, 4), f0, fn, True)
                pairs = ((to_right, to_right), (to_left, to_left))
        out = []
        for way, (src, dst) in enumerate(pairs):
            out.append(pltpu.make_async_remote_copy(
                src_ref=src, dst_ref=dst,
                send_sem=send_sem.at[par, q, 2 * c + way], recv_sem=recv_sem.at[par, q, 2 * c + way],
                device_id=(right[d], left[d])[way], device_id_type=MESH))
        return out

    def send(q, s):
        for c in range(3):
            for cp in copies(q, s, c):
                cp.start()

    def wait(q, s):
        for c in range(3):
            for cp in copies(q, s, c):
                cp.wait()

    def add_first(level, s):
        par = lax.rem(s, 2)
        (f0, fn), (s0, sn) = HALVES[level]
        for c in range(3):
            i = coord[(c + level) % 3]
            one = rows(level, s, c, lax.rem(i + 1, 4), f0, fn)
            one[...] = one[...] + ra[level][par, c, 0, 0:fn, :]
            two = rows(level, s, c, lax.rem(i + 3, 4), s0, sn)
            two[...] = two[...] + ra[level][par, c, 1, 0:sn, :]

    def add_second(level, s):
        par = lax.rem(s, 2)
        for c in range(3):
            i = coord[(c + level) % 3]
            own = rows(level, s, c, i, 0, BLK[level])
            total = own[...] + rb[level][par, c, 0] + rb[level][par, c, 1]
            if level == 1:
                l3[par, c, 0:56, :] = total
                l3[par, c, 56:64, :] = jnp.zeros((8, SLAB), F32)
            else:
                rows(level, s, c, i, 0, BLK[level], True)[...] = total

    mine_r = pl.ds(pl.multiple_of(core * ROWS, 8), ROWS)
    theirs_r = pl.ds(pl.multiple_of((1 - core) * ROWS, 8), ROWS)

    def swap(s):
        par = lax.rem(s, 2)
        return [pltpu.make_async_remote_copy(
            src_ref=slab.at[s, c, theirs_r, :], dst_ref=xb.at[par, c],
            send_sem=xs_sem.at[par, c], recv_sem=xr_sem.at[par, c], device_id=peer, device_id_type=MESH)
            for c in range(2)]

    def stage(j, s):
        if j == 13:
            for c, cp in enumerate(swap(s)):
                cp.wait()
                slab[s, c, theirs_r, :] = xb[lax.rem(s, 2), c]
            return
        if j > 0:
            wait(j - 1, s)
        if j in (1, 3, 5):
            add_first(j // 2, s)
        if j in (2, 4, 6):
            add_second(j // 2 - 1, s)
        if j == 8:
            for c in range(3):
                own = rows(1, s, c, coord[(c + 1) % 3], 0, BLK[1])
                own[...] = l3g[lax.rem(s, 3), c, 0:56, :]
        if j < 12:
            send(j, s)
        else:
            for cp in swap(s):
                cp.start()
            for i in range(D // SLAB):
                at = slice(i * SLAB, (i + 1) * SLAB)
                slab[s, 2, at, :] = slab[s, 2, at, :].T

    mine_w = pl.ds(pl.multiple_of(core * ROWS, 16), ROWS)
    theirs_w = pl.ds(pl.multiple_of((1 - core) * ROWS, 16), ROWS)

    def w_own(k, size):
        par = lax.rem(k, 2)
        off = pl.multiple_of(k * CHUNK, 128)
        at = pl.multiple_of(core * HALF + k * CHUNK, 128)
        return [
            pltpu.make_async_copy(w1_ref.at[:, pl.ds(at, size)], w1_v.at[par, mine_w, pl.ds(0, size)], w_sem.at[par, 0]),
            pltpu.make_async_copy(w3_ref.at[:, pl.ds(at, size)], w3_v.at[par, mine_w, pl.ds(0, size)], w_sem.at[par, 1]),
            pltpu.make_async_copy(w2_ref.at[pl.ds(off, size), :], w2_v.at[par, pl.ds(0, size), :], w_sem.at[par, 2]),
        ]

    def w_peer(k, size):
        par = lax.rem(k, 2)
        off = pl.multiple_of(k * CHUNK, 128)
        return [
            pltpu.make_async_copy(wx_ref.at[0, :, pl.ds(off, size)], w1_v.at[par, theirs_w, pl.ds(0, size)], w_sem.at[par, 3]),
            pltpu.make_async_copy(wx_ref.at[1, :, pl.ds(off, size)], w3_v.at[par, theirs_w, pl.ds(0, size)], w_sem.at[par, 4]),
        ]

    def x_copies(k, size):
        off = pl.multiple_of(k * CHUNK, 128)
        at = pl.multiple_of((1 - core) * HALF + k * CHUNK, 128)
        return [pltpu.make_async_remote_copy(
            src_ref=w_ref.at[:, pl.ds(at, size)], dst_ref=wx_ref.at[m, :, pl.ds(off, size)],
            send_sem=ws_sem.at[k, m], recv_sem=wr_sem.at[k, m], device_id=peer, device_id_type=MESH)
            for m, w_ref in ((0, w1_ref), (1, w3_ref))]

    first_at = pl.multiple_of((1 - core) * HALF, 128)
    x_first = [pltpu.make_async_remote_copy(
        src_ref=w_ref.at[:, pl.ds(first_at, CHUNK)], dst_ref=w_v.at[0, mine_w, :],
        send_sem=ws_sem.at[0, m], recv_sem=wr_sem.at[0, m], device_id=peer, device_id_type=MESH)
        for m, w_ref, w_v in ((0, w1_ref, w1_v), (1, w3_ref, w3_v))]

    own_tok = pl.ds(pl.multiple_of(core * TOK, TOK), TOK)
    own_h = pltpu.make_async_copy(h_ref, n_v.at[own_tok, :], in_sem.at[0])
    own_g = pltpu.make_async_copy(g_ref, gb_v.at[own_tok, :], in_sem.at[1])
    own_h.start()
    for cp in w_own(0, CHUNK):
        cp.start()
    own_g.start()

    barrier = pltpu.get_barrier_semaphore()
    for dev in right + left + [peer]:
        pl.semaphore_signal(barrier, inc=1, device_id=dev, device_id_type=MESH)
    pl.semaphore_wait(barrier, 7)

    peer_h = pltpu.make_async_remote_copy(
        src_ref=h_ref, dst_ref=n_v.at[own_tok, :], send_sem=is_sem.at[0], recv_sem=ir_sem.at[0],
        device_id=peer, device_id_type=MESH)
    peer_g = pltpu.make_async_remote_copy(
        src_ref=g_ref, dst_ref=gb_v.at[own_tok, :], send_sem=is_sem.at[1], recv_sem=ir_sem.at[1],
        device_id=peer, device_id_type=MESH)
    for cp in x_first:
        cp.start()
    peer_h.start()
    peer_g.start()

    def push(k, _):
        for cp in x_copies(k, CHUNK):
            cp.start()
        return 0

    lax.fori_loop(1, N_CHUNK - 1, push, 0)
    for cp in x_copies(N_CHUNK - 1, LAST):
        cp.start()

    def zero(m, _):
        dn_v[pl.ds(pl.multiple_of(m * 64, 64), 64), :] = jnp.zeros((64, D), F32)
        return 0

    lax.fori_loop(0, 2 * TOK // 64, zero, 0)

    def norm(base):
        def body(m, _):
            at = pl.multiple_of(base + m * 128, 128)
            hf = n_v[pl.ds(at, 128), :].astype(F32)
            inv = lax.rsqrt(jnp.mean(hf * hf, axis=-1, keepdims=True) + NORM_EPS)
            nb = (hf * inv).astype(BF16)
            n_v[pl.ds(at, 128), :] = nb
            nt_v[:, pl.ds(at, 128)] = nb.T
            return 0
        lax.fori_loop(0, TOK // 128, body, 0)

    def flip(base):
        def body(m, _):
            at = pl.multiple_of(base + m * 128, 128)
            gt_v[:, pl.ds(at, 128)] = gb_v[pl.ds(at, 128), :].T
            return 0
        lax.fori_loop(0, TOK // 128, body, 0)

    def w_fetch(k, size):
        for cp in w_own(k, size):
            cp.start()
        for cp in x_copies(k, size):
            cp.wait()
        for cp in w_peer(k, size):
            cp.start()

    def w_wait(k, size):
        for cp in w_own(k, size) + w_peer(k, size):
            cp.wait()

    own_h.wait()
    norm(core * TOK)
    own_g.wait()
    flip(core * TOK)

    def phase_a1(k):
        par = lax.rem(k, 2)

        @pl.when(k == 0)
        def _():
            for cp in w_own(0, CHUNK) + x_first:
                cp.wait()

        @pl.when((k > 0) & (k < N_CHUNK - 1))
        def _():
            w_wait(k, CHUNK)

        @pl.when(k == N_CHUNK - 1)
        def _():
            w_wait(k, LAST)
            w1_v[par, :, LAST:] = jnp.zeros((D, CHUNK - LAST), BF16)
            w3_v[par, :, LAST:] = jnp.zeros((D, CHUNK - LAST), BF16)
            w2_v[par, LAST:, :] = jnp.zeros((CHUNK - LAST, D), BF16)

        def body(m, _):
            @pl.when((k == 0) & (m == TOK // TILE_1))
            def _():
                peer_h.wait()
                norm((1 - core) * TOK)
                peer_g.wait()
                flip((1 - core) * TOK)

            tile = lax.rem(m + core * (TOK // TILE_1), 2 * TOK // TILE_1)
            at = pl.ds(pl.multiple_of(tile * TILE_1, TILE_1), TILE_1)
            nb = n_v[at, :]
            pre_up = dot(nb, w1_v[par], ((1,), (0,)))
            pre_lin = dot(nb, w3_v[par], ((1,), (0,)))
            d_act = dot(gb_v[at, :], w2_v[par], ((1,), (1,)))
            sig = jax.nn.sigmoid(pre_up)
            up_act = pre_up * sig
            a_v[at, :] = (up_act * pre_lin).astype(BF16)
            du_v[at, :] = (d_act * pre_lin * sig * (1.0 + pre_up * (1.0 - sig))).astype(BF16)
            dv_v[at, :] = (d_act * up_act).astype(BF16)
            return 0

        lax.fori_loop(0, 2 * TOK // TILE_1, body, 0)

    def phase_a2(k):
        par = lax.rem(k, 2)

        def body(m, _):
            at = pl.ds(pl.multiple_of(m * TILE_2, TILE_2), TILE_2)
            dn_v[at, :] += dot(du_v[at, :], w1_v[par], ((1,), (1,))) + dot(dv_v[at, :], w3_v[par], ((1,), (1,)))
            return 0

        lax.fori_loop(0, 2 * TOK // TILE_2, body, 0)

    def phase_b(k):
        s0 = 2 * k
        s1 = 2 * k + 1 - lax.div(k, N_CHUNK - 1)

        def body(m, _):
            at = pl.ds(pl.multiple_of(m * TILE_B, 8), TILE_B)
            for c, (lhs, rhs) in enumerate(((nt_v, du_v), (nt_v, dv_v), (gt_v, a_v))):
                out = dot(lhs[at, :], rhs[...], ((1,), (0,)))
                slab[s1, c, at, :] = out[:, SLAB:]
                slab[s0, c, at, :] = out[:, :SLAB]
            return 0

        lax.fori_loop(0, D // TILE_B, body, 0)

    dn_copy = pltpu.make_async_remote_copy(
        src_ref=dn_v.at[pl.ds(pl.multiple_of((1 - core) * TOK, TOK), TOK), :], dst_ref=dnx_ref,
        send_sem=is_sem.at[2], recv_sem=ir_sem.at[2], device_id=peer, device_id_type=MESH)

    def fin_in(m):
        at = pl.ds(pl.multiple_of(m * TILE, TILE), TILE)
        return [pltpu.make_async_copy(dnx_ref.at[at, :], dnr_v, fin_sem.at[0]),
                pltpu.make_async_copy(h_ref.at[at, :], hr_v, fin_sem.at[1])]

    def final(m):
        for cp in fin_in(m):
            cp.wait()

        mine = pl.multiple_of(core * TOK + m * TILE, TILE)

        def body(p, _):
            sub = pl.ds(pl.multiple_of(p * 64, 64), 64)
            here = pl.ds(pl.multiple_of(mine + p * 64, 64), 64)
            hf = hr_v[sub, :].astype(F32)
            inv = lax.rsqrt(jnp.mean(hf * hf, axis=-1, keepdims=True) + NORM_EPS)
            y = hf * inv
            d_norm = dn_v[here, :] + dnr_v[sub, :]
            d_h = inv * (d_norm - y * jnp.mean(d_norm * y, axis=-1, keepdims=True))
            oh_ref[pl.ds(pl.multiple_of(m * TILE + p * 64, 64), 64), :] = (gb_v[here, :].astype(F32) + d_h).astype(BF16)
            return 0

        lax.fori_loop(0, TILE // 64, body, 0)

        @pl.when(m < TOK // TILE - 1)
        def _():
            for cp in fin_in(m + 1):
                cp.start()

    def step(tt, _):
        k = lax.div(tt, 2)
        odd = lax.rem(tt, 2)

        @pl.when((odd == 0) & (k > 0) & (k <= N_CHUNK))
        def _():
            phase_a2(k - 1)

        @pl.when((tt == 1) | ((odd == 0) & (k > 0) & (k < N_CHUNK - 2)))
        def _():
            w_fetch(k + 1, CHUNK)

        @pl.when((odd == 0) & (k == N_CHUNK - 2))
        def _():
            w_fetch(k + 1, LAST)

        @pl.when((odd == 0) & (k < N_CHUNK))
        def _():
            phase_a1(k)

        @pl.when((odd == 1) & (k < N_CHUNK))
        def _():
            phase_b(k)

        @pl.when(tt == 2 * N_CHUNK)
        def _():
            dn_copy.start()

        @pl.when(tt == FIN - 1)
        def _():
            dn_copy.wait()
            for cp in fin_in(0):
                cp.start()

        @pl.when((tt >= FIN) & (tt < FIN + TOK // TILE))
        def _():
            final(tt - FIN)

        for j in reversed(range(N_STAGE)):
            s = tt - 1 - j

            @pl.when((s >= 0) & (s < N_SLAB))
            def _(j=j, s=s):
                stage(j, s)

        return 0

    lax.fori_loop(0, N_SLAB + N_STAGE, step, 0)


def store_kernel(slab, h_v, o1_ref, o3_ref, o2_ref, oh_ref, sem, h_sem):
    core = lax.axis_index("fsdp")

    def copies(s):
        out = []
        for half, who in enumerate((core, 1 - core)):
            part = pl.ds(pl.multiple_of(who * ROWS, 8), ROWS)
            cols = pl.ds(pl.multiple_of(who * HALF + s * SLAB, 128), SLAB)
            for c, o_ref in ((0, o1_ref), (1, o3_ref)):
                out.append(pltpu.make_async_copy(slab.at[s, c, part, :], o_ref.at[:, cols], sem.at[s, 2 * half + c]))
        to = pl.ds(pl.multiple_of(s * SLAB, 128), SLAB)
        for i in range(D // SLAB):
            at = pl.ds(i * SLAB, SLAB)
            out.append(pltpu.make_async_copy(slab.at[s, 2, at, :], o2_ref.at[to, at], sem.at[s, 4 + i]))
        return out

    def start(s, _):
        for cp in copies(s):
            cp.start()
        return 0

    def wait(s, _):
        for cp in copies(s):
            cp.wait()
        return 0

    h_copy = pltpu.make_async_copy(h_v, oh_ref, h_sem.at[0])
    h_copy.start()
    lax.fori_loop(0, N_SLAB, start, 0)
    lax.fori_loop(0, N_SLAB, wait, 0)
    h_copy.wait()


def solution(mesh):
    tok_spec = P(('replica', 'fsdp'), None)
    act_spec = P(None, ('replica', 'fsdp'), None)
    weight_spec = P(None, 'fsdp', None)

    def local_step(block_in, grad_out, w_up, w_lin, w_down):
        any_spec = pl.BlockSpec(memory_space=pl.ANY)
        dma = pltpu.SemaphoreType.DMA
        vmem_spec = pl.BlockSpec(memory_space=pltpu.VMEM)
        sums, oh, _, _ = pl.pallas_call(
            kernel,
            out_shape=(
                pltpu.VMEM((N_SLAB, 3, D, SLAB), F32),
                pltpu.VMEM((TOK, D), BF16),
                jax.ShapeDtypeStruct((2, ROWS, HALF), BF16),
                jax.ShapeDtypeStruct((TOK, D), F32),
            ),
            in_specs=[any_spec] * 5,
            out_specs=(vmem_spec, vmem_spec, any_spec, any_spec),
            scratch_shapes=[
                pltpu.VMEM((2, 3, 64, SLAB), F32),
                pltpu.VMEM((3, 3, 64, SLAB), F32),
                pltpu.VMEM((2, 3, 2, 112, SLAB), F32),
                pltpu.VMEM((2, 3, 2, 224, SLAB), F32),
                pltpu.VMEM((2, 3, 2, 32, SLAB), F32),
                pltpu.VMEM((2, 3, 2, 56, SLAB), F32),
                pltpu.VMEM((2, 3, 2, 8, SLAB), F32),
                pltpu.VMEM((2, 3, 2, 16, SLAB), F32),
                pltpu.VMEM((2 * TOK, D), BF16),
                pltpu.VMEM((D, 2 * TOK), BF16),
                pltpu.VMEM((2 * TOK, D), BF16),
                pltpu.VMEM((D, 2 * TOK), BF16),
                pltpu.VMEM((2 * TOK, D), F32),
                pltpu.VMEM((2 * TOK, CHUNK), BF16),
                pltpu.VMEM((2 * TOK, CHUNK), BF16),
                pltpu.VMEM((2 * TOK, CHUNK), BF16),
                pltpu.VMEM((2, D, CHUNK), BF16),
                pltpu.VMEM((2, D, CHUNK), BF16),
                pltpu.VMEM((2, CHUNK, D), BF16),
                pltpu.VMEM((2, 2, ROWS, SLAB), F32),
                pltpu.VMEM((TILE, D), F32),
                pltpu.VMEM((TILE, D), BF16),
                dma((2, 12, 6)),
                dma((2, 12, 6)),
                dma((2, 2)),
                dma((2, 2)),
                dma((2, 5)),
                dma((N_CHUNK, 2)),
                dma((N_CHUNK, 2)),
                dma((2,)),
                dma((3,)),
                dma((3,)),
                dma((3,)),
            ],
            compiler_params=pltpu.CompilerParams(
                collective_id=0, has_side_effects=True, vmem_limit_bytes=39000000),
        )(block_in[0], grad_out, w_up[0], w_lin[0], w_down[0])
        o1, o3, o2, oh = pl.pallas_call(
            store_kernel,
            out_shape=(
                jax.ShapeDtypeStruct((ROWS, FF), F32),
                jax.ShapeDtypeStruct((ROWS, FF), F32),
                jax.ShapeDtypeStruct((HALF, D), F32),
                jax.ShapeDtypeStruct((TOK, D), BF16),
            ),
            in_specs=[vmem_spec] * 2,
            out_specs=(any_spec,) * 4,
            scratch_shapes=[dma((N_SLAB, 4 + D // SLAB)), dma((1,))],
            compiler_params=pltpu.CompilerParams(has_side_effects=True, vmem_limit_bytes=1048576),
        )(sums, oh)
        return o1[None], o3[None], o2[None], oh

    return jax.shard_map(local_step, mesh=mesh, in_specs=(act_spec, tok_spec, weight_spec, weight_spec, weight_spec), out_specs=(weight_spec, weight_spec, weight_spec, tok_spec), check_vma=False)
```

time: 309 us -> 256 us (0.83)
  Pallas kernels: 289 us -> 256 us
  local copies, waits for them, and re-layouts: 19.5 us -> 0 us
    pallas_call x1 -> x2, Pallas kernels: 289 us -> 256 us  [the longest x1 245 us: local_step(): pl.pallas_call(kernel, out_shape=(pltpu.VMEM((N_SLAB, 3, D, SLAB), F32),...]
    unnamed x14 -> x0, local copies, waits for them, and re-layouts: 19.5 us -> none
where the time goes in v2:
time: 256 us
  Pallas kernels  256 us (100%)
    pallas_call x1, Pallas kernels, local_step(): pl.pallas_call(kernel, out_shape=(pltpu.VMEM((N_SLAB, 3, D, SLAB), F32),...  245 us
    pallas_call x1, Pallas kernels, local_step(): pl.pallas_call(store_kernel, out_shape=(jax.ShapeDtypeStruct((ROWS, FF),...  11 us

profile of v2, /device:TPU:1, one launch (start us, length us, event | category | flops | bytes accessed | tf_op | source)
XLA Modules:
  0.0 256.3 jit_solution(7540215256681941269)
XLA Ops:
  0.6 244.6 %shard_map.84 = (f32[19,3,896,128]{3,2,1,0:T(8,128)S(1)}, bf16[1024,896]{1,0:T(8,128)(2,1)S(1)}, bf16[2,448,2432]{2,1,0:T(8,128)(2,1)}, f32[1024,896]{1,0:T(8,128)}) custom-call(bf16[1024,896]{1,0:T(8,128)(2,1)} %bitcast.10, bf16[1024,896]{1,0:T(8,128)(2,1)} %g_ref.1, bf16[448,4864]{1,0:T(8,128)(2,1)} %bitcast.7, bf16[448,4864]{1,0:T(8,128)(2,1)} %bitcast.8, ...), custom_call_target="tpu_custom_call" | custom-call | tf_op jit(solution)/shard_map/pallas_call | solution.py:465
  245.3 11.0 %shard_map.85 = (f32[448,4864]{1,0:T(8,128)}, f32[448,4864]{1,0:T(8,128)}, f32[2432,896]{1,0:T(8,128)}, bf16[1024,896]{1,0:T(8,128)(2,1)}) custom-call(f32[19,3,896,128]{3,2,1,0:T(8,128)S(1)} %get-tuple-element.10.slab, bf16[1024,896]{1,0:T(8,128)(2,1)S(1)} %get-tuple-element.11.h_v), custom_call_target="tpu_custom_call" | custom-call | tf_op jit(solution)/shard_map/pallas_call | solution.py:513

commit v3 on v2

--- a/solution.py
+++ b/solution.py
@@ -22,12 +22,16 @@
 ROWS = D // 2
 TILE = 128
 TILE_1 = 512
-TILE_2 = 1024
+TILE_2 = 512
 TILE_B = 128
 BLK = (224, 56, 16)
 HALVES = (((0, 112), (112, 112)), ((0, 32), (32, 24)), ((0, 8), (8, 8)))
-N_STAGE = 14
-FIN = 2 * N_CHUNK + 4
+OFFSET = (0, 2, 4, 5, 6, 7, 8, 9, 10, 11, 12, 14, 16, 17)
+N_STAGE = len(OFFSET)
+SLOTS_A = (4, 2, 2)
+SLOTS_B = (3, 2, 2)
+A2 = 2 * N_CHUNK + 1
+FIN = A2 + N_CHUNK + 2
 
 
 def dot(a, b, dims):
@@ -35,10 +39,10 @@
 
 
 def kernel(h_ref, g_ref, w1_ref, w3_ref, w2_ref,
-           slab, oh_ref, wx_ref, dnx_ref,
+           slab, oh_ref, wx_ref, dnx_ref, dux_ref,
            l3, l3g, ra0, rb0, ra1, rb1, ra2, rb2,
-           n_v, nt_v, gb_v, gt_v, dn_v, a_v, du_v, dv_v, w1_v, w3_v, w2_v, xb, dnr_v, hr_v,
-           send_sem, recv_sem, xs_sem, xr_sem, w_sem, ws_sem, wr_sem, in_sem, is_sem, ir_sem, fin_sem):
+           n_v, nt_v, gb_v, gt_v, dn_v, a_v, du_v, dv_v, w1_v, w3_v, w2_v, xb, dnr_v,
+           send_sem, recv_sem, xs_sem, xr_sem, w_sem, ws_sem, wr_sem, in_sem, is_sem, ir_sem, fin_sem, du_sem):
     rep = lax.axis_index("replica")
     core = lax.axis_index("fsdp")
     coord = (lax.rem(rep, 4), lax.rem(lax.div(rep, 4), 4), lax.div(rep, 16))
@@ -62,7 +66,7 @@
         return ref.at[s, c, pl.ds(pl.multiple_of(base, 8), size), :]
 
     def copies(q, s, c):
-        par = lax.rem(s, 2)
+        par = lax.rem(s, 4)
         if q < 6:
             level, second, gather = q // 2, q % 2, False
         else:
@@ -74,11 +78,13 @@
         if not gather:
             if second == 0:
                 b = lax.rem(i + 2, 4)
-                pairs = ((rows(level, s, c, b, f0, fn), ra[level].at[par, c, 0, pl.ds(0, fn), :]),
-                         (rows(level, s, c, b, s0, sn), ra[level].at[par, c, 1, pl.ds(0, sn), :]))
+                at = lax.rem(s, SLOTS_A[level])
+                pairs = ((rows(level, s, c, b, f0, fn), ra[level].at[at, c, 0, pl.ds(0, fn), :]),
+                         (rows(level, s, c, b, s0, sn), ra[level].at[at, c, 1, pl.ds(0, sn), :]))
             else:
-                pairs = ((rows(level, s, c, lax.rem(i + 1, 4), 0, blk), rb[level].at[par, c, 0]),
-                         (rows(level, s, c, lax.rem(i + 3, 4), 0, blk), rb[level].at[par, c, 1]))
+                at = lax.rem(s, SLOTS_B[level])
+                pairs = ((rows(level, s, c, lax.rem(i + 1, 4), 0, blk), rb[level].at[at, c, 0]),
+                         (rows(level, s, c, lax.rem(i + 3, 4), 0, blk), rb[level].at[at, c, 1]))
         else:
             if second == 0:
                 own = rows(level, s, c, i, 0, blk, True)
@@ -106,7 +112,7 @@
                 cp.wait()
 
     def add_first(level, s):
-        par = lax.rem(s, 2)
+        par = lax.rem(s, SLOTS_A[level])
         (f0, fn), (s0, sn) = HALVES[level]
         for c in range(3):
             i = coord[(c + level) % 3]
@@ -116,11 +122,12 @@
             two[...] = two[...] + ra[level][par, c, 1, 0:sn, :]
 
     def add_second(level, s):
+        at = lax.rem(s, SLOTS_B[level])
         par = lax.rem(s, 2)
         for c in range(3):
             i = coord[(c + level) % 3]
             own = rows(level, s, c, i, 0, BLK[level])
-            total = own[...] + rb[level][par, c, 0] + rb[level][par, c, 1]
+            total = own[...] + rb[level][at, c, 0] + rb[level][at, c, 1]
             if level == 1:
                 l3[par, c, 0:56, :] = total
                 l3[par, c, 56:64, :] = jnp.zeros((8, SLAB), F32)
@@ -165,15 +172,17 @@
     mine_w = pl.ds(pl.multiple_of(core * ROWS, 16), ROWS)
     theirs_w = pl.ds(pl.multiple_of((1 - core) * ROWS, 16), ROWS)
 
-    def w_own(k, size):
+    def w_own(k, size, down=True):
         par = lax.rem(k, 2)
         off = pl.multiple_of(k * CHUNK, 128)
         at = pl.multiple_of(core * HALF + k * CHUNK, 128)
-        return [
+        out = [
             pltpu.make_async_copy(w1_ref.at[:, pl.ds(at, size)], w1_v.at[par, mine_w, pl.ds(0, size)], w_sem.at[par, 0]),
             pltpu.make_async_copy(w3_ref.at[:, pl.ds(at, size)], w3_v.at[par, mine_w, pl.ds(0, size)], w_sem.at[par, 1]),
-            pltpu.make_async_copy(w2_ref.at[pl.ds(off, size), :], w2_v.at[par, pl.ds(0, size), :], w_sem.at[par, 2]),
         ]
+        if down:
+            out.append(pltpu.make_async_copy(w2_ref.at[pl.ds(off, size), :], w2_v.at[par, pl.ds(0, size), :], w_sem.at[par, 2]))
+        return out
 
     def w_peer(k, size):
         par = lax.rem(k, 2)
@@ -194,7 +203,7 @@
     first_at = pl.multiple_of((1 - core) * HALF, 128)
     x_first = [pltpu.make_async_remote_copy(
         src_ref=w_ref.at[:, pl.ds(first_at, CHUNK)], dst_ref=w_v.at[0, mine_w, :],
-        send_sem=ws_sem.at[0, m], recv_sem=wr_sem.at[0, m], device_id=peer, device_id_type=MESH)
+        send_sem=ws_sem.at[N_CHUNK, m], recv_sem=wr_sem.at[N_CHUNK, m], device_id=peer, device_id_type=MESH)
         for m, w_ref, w_v in ((0, w1_ref, w1_v), (1, w3_ref, w3_v))]
 
     own_tok = pl.ds(pl.multiple_of(core * TOK, TOK), TOK)
@@ -227,7 +236,7 @@
         return 0
 
     lax.fori_loop(1, N_CHUNK - 1, push, 0)
-    for cp in x_copies(N_CHUNK - 1, LAST):
+    for cp in x_copies(N_CHUNK - 1, LAST) + x_copies(0, CHUNK):
         cp.start()
 
     def zero(m, _):
@@ -313,8 +322,26 @@
 
         lax.fori_loop(0, 2 * TOK // TILE_1, body, 0)
 
+    def du_save(k):
+        return [pltpu.make_async_copy(du_v, dux_ref.at[k, 0], du_sem.at[0]),
+                pltpu.make_async_copy(dv_v, dux_ref.at[k, 1], du_sem.at[1])]
+
+    def a2_copies(k, size):
+        return [pltpu.make_async_copy(dux_ref.at[k, 0], du_v, du_sem.at[0]),
+                pltpu.make_async_copy(dux_ref.at[k, 1], dv_v, du_sem.at[1])] + w_own(k, size, False) + w_peer(k, size)
+
     def phase_a2(k):
         par = lax.rem(k, 2)
+
+        @pl.when(k < N_CHUNK - 1)
+        def _():
+            for cp in a2_copies(k, CHUNK):
+                cp.wait()
+
+        @pl.when(k == N_CHUNK - 1)
+        def _():
+            for cp in a2_copies(k, LAST):
+                cp.wait()
 
         def body(m, _):
             at = pl.ds(pl.multiple_of(m * TILE_2, TILE_2), TILE_2)
@@ -342,9 +369,10 @@
         send_sem=is_sem.at[2], recv_sem=ir_sem.at[2], device_id=peer, device_id_type=MESH)
 
     def fin_in(m):
-        at = pl.ds(pl.multiple_of(m * TILE, TILE), TILE)
-        return [pltpu.make_async_copy(dnx_ref.at[at, :], dnr_v, fin_sem.at[0]),
-                pltpu.make_async_copy(h_ref.at[at, :], hr_v, fin_sem.at[1])]
+        return [pltpu.make_async_copy(
+            dnx_ref.at[pl.ds(pl.multiple_of((m + e) * TILE, TILE), TILE), :], dnr_v.at[e], fin_sem.at[e]) for e in range(2)]
+
+    h_again = pltpu.make_async_copy(h_ref, n_v.at[own_tok, :], fin_sem.at[2])
 
     def final(m):
         for cp in fin_in(m):
@@ -353,21 +381,21 @@
         mine = pl.multiple_of(core * TOK + m * TILE, TILE)
 
         def body(p, _):
-            sub = pl.ds(pl.multiple_of(p * 64, 64), 64)
+            sub = pl.ds(pl.multiple_of(lax.rem(p, TILE // 64) * 64, 64), 64)
             here = pl.ds(pl.multiple_of(mine + p * 64, 64), 64)
-            hf = hr_v[sub, :].astype(F32)
+            hf = n_v[here, :].astype(F32)
             inv = lax.rsqrt(jnp.mean(hf * hf, axis=-1, keepdims=True) + NORM_EPS)
             y = hf * inv
-            d_norm = dn_v[here, :] + dnr_v[sub, :]
+            d_norm = dn_v[here, :] + dnr_v[lax.div(p, TILE // 64), sub, :]
             d_h = inv * (d_norm - y * jnp.mean(d_norm * y, axis=-1, keepdims=True))
             oh_ref[pl.ds(pl.multiple_of(m * TILE + p * 64, 64), 64), :] = (gb_v[here, :].astype(F32) + d_h).astype(BF16)
             return 0
 
-        lax.fori_loop(0, TILE // 64, body, 0)
-
-        @pl.when(m < TOK // TILE - 1)
-        def _():
-            for cp in fin_in(m + 1):
+        lax.fori_loop(0, 2 * TILE // 64, body, 0)
+
+        @pl.when(m < TOK // TILE - 2)
+        def _():
+            for cp in fin_in(m + 2):
                 cp.start()
 
     def step(tt, _):
@@ -376,7 +404,8 @@
 
         @pl.when((odd == 0) & (k > 0) & (k <= N_CHUNK))
         def _():
-            phase_a2(k - 1)
+            for cp in du_save(k - 1):
+                cp.wait()
 
         @pl.when((tt == 1) | ((odd == 0) & (k > 0) & (k < N_CHUNK - 2)))
         def _():
@@ -389,27 +418,50 @@
         @pl.when((odd == 0) & (k < N_CHUNK))
         def _():
             phase_a1(k)
+            for cp in du_save(k):
+                cp.start()
 
         @pl.when((odd == 1) & (k < N_CHUNK))
         def _():
             phase_b(k)
 
-        @pl.when(tt == 2 * N_CHUNK)
+        @pl.when((tt >= A2) & (tt < A2 + N_CHUNK))
+        def _():
+            phase_a2(tt - A2)
+
+        @pl.when(tt == A2 - 1)
+        def _():
+            for cp in x_copies(0, CHUNK):
+                cp.wait()
+
+        @pl.when((tt >= A2 - 1) & (tt < A2 + N_CHUNK - 2))
+        def _():
+            for cp in a2_copies(tt - A2 + 1, CHUNK):
+                cp.start()
+
+        @pl.when(tt == A2 + N_CHUNK - 2)
+        def _():
+            for cp in a2_copies(N_CHUNK - 1, LAST):
+                cp.start()
+
+        @pl.when(tt == A2 + N_CHUNK - 1)
         def _():
             dn_copy.start()
+            h_again.start()
 
         @pl.when(tt == FIN - 1)
         def _():
             dn_copy.wait()
+            h_again.wait()
             for cp in fin_in(0):
                 cp.start()
 
-        @pl.when((tt >= FIN) & (tt < FIN + TOK // TILE))
-        def _():
-            final(tt - FIN)
+        @pl.when((tt >= FIN) & (tt < FIN + TOK // TILE // 2))
+        def _():
+            final(2 * (tt - FIN))
 
         for j in reversed(range(N_STAGE)):
-            s = tt - 1 - j
+            s = tt - 1 - OFFSET[j]
 
             @pl.when((s >= 0) & (s < N_SLAB))
             def _(j=j, s=s):
@@ -417,7 +469,7 @@
 
         return 0
 
-    lax.fori_loop(0, N_SLAB + N_STAGE, step, 0)
+    lax.fori_loop(0, N_SLAB + OFFSET[-1] + 1, step, 0)
 
 
 def store_kernel(slab, h_v, o1_ref, o3_ref, o2_ref, oh_ref, sem, h_sem):
@@ -462,21 +514,22 @@
         any_spec = pl.BlockSpec(memory_space=pl.ANY)
         dma = pltpu.SemaphoreType.DMA
         vmem_spec = pl.BlockSpec(memory_space=pltpu.VMEM)
-        sums, oh, _, _ = pl.pallas_call(
+        sums, oh, _, _, _ = pl.pallas_call(
             kernel,
             out_shape=(
                 pltpu.VMEM((N_SLAB, 3, D, SLAB), F32),
                 pltpu.VMEM((TOK, D), BF16),
                 jax.ShapeDtypeStruct((2, ROWS, HALF), BF16),
                 jax.ShapeDtypeStruct((TOK, D), F32),
+                jax.ShapeDtypeStruct((N_CHUNK, 2, 2 * TOK, CHUNK), BF16),
             ),
             in_specs=[any_spec] * 5,
-            out_specs=(vmem_spec, vmem_spec, any_spec, any_spec),
+            out_specs=(vmem_spec, vmem_spec, any_spec, any_spec, any_spec),
             scratch_shapes=[
                 pltpu.VMEM((2, 3, 64, SLAB), F32),
                 pltpu.VMEM((3, 3, 64, SLAB), F32),
-                pltpu.VMEM((2, 3, 2, 112, SLAB), F32),
-                pltpu.VMEM((2, 3, 2, 224, SLAB), F32),
+                pltpu.VMEM((SLOTS_A[0], 3, 2, 112, SLAB), F32),
+                pltpu.VMEM((SLOTS_B[0], 3, 2, 224, SLAB), F32),
                 pltpu.VMEM((2, 3, 2, 32, SLAB), F32),
                 pltpu.VMEM((2, 3, 2, 56, SLAB), F32),
                 pltpu.VMEM((2, 3, 2, 8, SLAB), F32),
@@ -493,19 +546,19 @@
                 pltpu.VMEM((2, D, CHUNK), BF16),
                 pltpu.VMEM((2, CHUNK, D), BF16),
                 pltpu.VMEM((2, 2, ROWS, SLAB), F32),
-                pltpu.VMEM((TILE, D), F32),
-                pltpu.VMEM((TILE, D), BF16),
-                dma((2, 12, 6)),
-                dma((2, 12, 6)),
+                pltpu.VMEM((2, TILE, D), F32),
+                dma((4, 12, 6)),
+                dma((4, 12, 6)),
                 dma((2, 2)),
                 dma((2, 2)),
                 dma((2, 5)),
-                dma((N_CHUNK, 2)),
-                dma((N_CHUNK, 2)),
+                dma((N_CHUNK + 1, 2)),
+                dma((N_CHUNK + 1, 2)),
                 dma((2,)),
                 dma((3,)),
                 dma((3,)),
                 dma((3,)),
+                dma((2,)),
             ],
             compiler_params=pltpu.CompilerParams(
                 collective_id=0, has_side_effects=True, vmem_limit_bytes=39000000),

time: 256 us -> 245 us (0.957)
  Pallas kernels: 256 us -> 244 us
    pallas_call x1, Pallas kernels: 245 us -> 233 us  [local_step(): pl.pallas_call(kernel, out_shape=(pltpu.VMEM((N_SLAB, 3, D, SLAB), F32),...]
where the time goes in v3:
time: 245 us
  Pallas kernels  244 us (100%)
    pallas_call x1, Pallas kernels, local_step(): pl.pallas_call(kernel, out_shape=(pltpu.VMEM((N_SLAB, 3, D, SLAB), F32),...  233 us
    pallas_call x1, Pallas kernels, local_step(): pl.pallas_call(store_kernel, out_shape=(jax.ShapeDtypeStruct((ROWS, FF),...  11 us

profile of v3, /device:TPU:1, one launch (start us, length us, event | category | flops | bytes accessed | tf_op | source)
XLA Modules:
  0.0 244.8 jit_solution(3116295090358971228)
XLA Ops:
  0.6 233.2 %shard_map.84 = (f32[19,3,896,128]{3,2,1,0:T(8,128)S(1)}, bf16[1024,896]{1,0:T(8,128)(2,1)S(1)}, bf16[2,448,2432]{2,1,0:T(8,128)(2,1)}, f32[1024,896]{1,0:T(8,128)}, bf16[10,2,2048,256]{3,2,1,0:T(8,128)(2,1)}) custom-call(bf16[1024,896]{1,0:T(8,128)(2,1)} %bitcast.10, bf16[1024,896]{1,0:T(8,128)(2,1)} %g_ref.1, bf16[448,4864]{1,0:T(8,128)(2,1)} %bitcast.7, ...), custom_call_target="tpu_custom_call" | custom-call | tf_op jit(solution)/shard_map/pallas_call | solution.py:517
  233.8 11.0 %shard_map.85 = (f32[448,4864]{1,0:T(8,128)}, f32[448,4864]{1,0:T(8,128)}, f32[2432,896]{1,0:T(8,128)}, bf16[1024,896]{1,0:T(8,128)(2,1)}) custom-call(f32[19,3,896,128]{3,2,1,0:T(8,128)S(1)} %get-tuple-element.10.slab, bf16[1024,896]{1,0:T(8,128)(2,1)S(1)} %get-tuple-element.11.h_v), custom_call_target="tpu_custom_call" | custom-call | tf_op jit(solution)/shard_map/pallas_call | solution.py:566

commit v4 on v3

--- a/solution.py
+++ b/solution.py
@@ -27,11 +27,11 @@
 BLK = (224, 56, 16)
 HALVES = (((0, 112), (112, 112)), ((0, 32), (32, 24)), ((0, 8), (8, 8)))
 OFFSET = (0, 2, 4, 5, 6, 7, 8, 9, 10, 11, 12, 14, 16, 17)
-N_STAGE = len(OFFSET)
+ORDER = (9, 8, 7, 6, 5, 4, 3, 2, 13, 12, 11, 10, 1, 0)
 SLOTS_A = (4, 2, 2)
 SLOTS_B = (3, 2, 2)
-A2 = 2 * N_CHUNK + 1
-FIN = A2 + N_CHUNK + 2
+A2 = 2 * N_CHUNK
+FIN = A2 + N_CHUNK + 1
 
 
 def dot(a, b, dims):
@@ -243,8 +243,6 @@
         dn_v[pl.ds(pl.multiple_of(m * 64, 64), 64), :] = jnp.zeros((64, D), F32)
         return 0
 
-    lax.fori_loop(0, 2 * TOK // 64, zero, 0)
-
     def norm(base):
         def body(m, _):
             at = pl.multiple_of(base + m * 128, 128)
@@ -402,7 +400,7 @@
         k = lax.div(tt, 2)
         odd = lax.rem(tt, 2)
 
-        @pl.when((odd == 0) & (k > 0) & (k <= N_CHUNK))
+        @pl.when((odd == 0) & (k > 0) & (k < N_CHUNK))
         def _():
             for cp in du_save(k - 1):
                 cp.wait()
@@ -425,6 +423,11 @@
         def _():
             phase_b(k)
 
+        @pl.when(tt == 2 * N_CHUNK - 1)
+        def _():
+            for cp in du_save(N_CHUNK - 1):
+                cp.wait()
+
         @pl.when((tt >= A2) & (tt < A2 + N_CHUNK))
         def _():
             phase_a2(tt - A2)
@@ -433,6 +436,7 @@
         def _():
             for cp in x_copies(0, CHUNK):
                 cp.wait()
+            lax.fori_loop(0, 2 * TOK // 64, zero, 0)
 
         @pl.when((tt >= A2 - 1) & (tt < A2 + N_CHUNK - 2))
         def _():
@@ -460,7 +464,7 @@
         def _():
             final(2 * (tt - FIN))
 
-        for j in reversed(range(N_STAGE)):
+        for j in ORDER:
             s = tt - 1 - OFFSET[j]
 
             @pl.when((s >= 0) & (s < N_SLAB))
@@ -469,7 +473,7 @@
 
         return 0
 
-    lax.fori_loop(0, N_SLAB + OFFSET[-1] + 1, step, 0)
+    lax.fori_loop(0, max(N_SLAB + OFFSET[-1] + 1, FIN + TOK // TILE // 2), step, 0)
 
 
 def store_kernel(slab, h_v, o1_ref, o3_ref, o2_ref, oh_ref, sem, h_sem):

time: 245 us -> 240 us (0.980)
  Pallas kernels: 244 us -> 240 us
    pallas_call x1, Pallas kernels: 233 us -> 229 us  [local_step(): pl.pallas_call(kernel, out_shape=(pltpu.VMEM((N_SLAB, 3, D, SLAB), F32),...]
where the time goes in v4:
time: 240 us
  Pallas kernels  240 us (100%)
    pallas_call x1, Pallas kernels, local_step(): pl.pallas_call(kernel, out_shape=(pltpu.VMEM((N_SLAB, 3, D, SLAB), F32),...  229 us
    pallas_call x1, Pallas kernels, local_step(): pl.pallas_call(store_kernel, out_shape=(jax.ShapeDtypeStruct((ROWS, FF),...  11 us

profile of v4, /device:TPU:1, one launch (start us, length us, event | category | flops | bytes accessed | tf_op | source)
XLA Modules:
  0.0 240.2 jit_solution(3382703327123552724)
XLA Ops:
  0.6 228.6 %shard_map.84 = (f32[19,3,896,128]{3,2,1,0:T(8,128)S(1)}, bf16[1024,896]{1,0:T(8,128)(2,1)S(1)}, bf16[2,448,2432]{2,1,0:T(8,128)(2,1)}, f32[1024,896]{1,0:T(8,128)}, bf16[10,2,2048,256]{3,2,1,0:T(8,128)(2,1)}) custom-call(bf16[1024,896]{1,0:T(8,128)(2,1)} %bitcast.10, bf16[1024,896]{1,0:T(8,128)(2,1)} %g_ref.1, bf16[448,4864]{1,0:T(8,128)(2,1)} %bitcast.7, ...), custom_call_target="tpu_custom_call" | custom-call | tf_op jit(solution)/shard_map/pallas_call | solution.py:521
  229.2 11.0 %shard_map.85 = (f32[448,4864]{1,0:T(8,128)}, f32[448,4864]{1,0:T(8,128)}, f32[2432,896]{1,0:T(8,128)}, bf16[1024,896]{1,0:T(8,128)(2,1)}) custom-call(f32[19,3,896,128]{3,2,1,0:T(8,128)S(1)} %get-tuple-element.10.slab, bf16[1024,896]{1,0:T(8,128)(2,1)S(1)} %get-tuple-element.11.h_v), custom_call_target="tpu_custom_call" | custom-call | tf_op jit(solution)/shard_map/pallas_call | solution.py:570
